TPU v7x, 768 devices: a whole 4x8x12 slice. The times are simulated.
768 devices in a mesh: fsdp: 64 (over x, y, core), grp: 12 (over z).
Axes of the slice: x: 4, y: 8, z: 12, core: 2. Of those that a mesh axis runs over, the one named last changes fastest.
Arguments:
- grad_flat: bfloat16 [12, 32768, 256], P('grp', 'fsdp'), may hold values from -6 to 6
- row_block: int32 [12, 32768], P('grp', 'fsdp'), may hold values from 0 to 127, as said below
- row_index: int32 [12, 32768], P('grp', 'fsdp'), may hold values from 0 to 255
- block_home: int32 [12, 128], P('grp'), may hold values from 0 to 127, as said below
- cov_left: float32 [12, 128, 256, 256], P('grp', 'fsdp'), may hold values from -4 to 4
- cov_right: float32 [12, 128, 256, 256], P('grp', 'fsdp'), may hold values from -4 to 4
- basis_left: bfloat16 [12, 128, 256, 256], P('grp', 'fsdp'), may hold values from -0.375 to 0.375
- basis_right: bfloat16 [12, 128, 256, 256], P('grp', 'fsdp'), may hold values from -0.375 to 0.375
- moment_first: bfloat16 [12, 128, 256, 256], P('grp', 'fsdp'), may hold values from -0.59765625 to 0.59765625
- moment_second: bfloat16 [12, 128, 256, 256], P('grp', 'fsdp'), may hold values from 0.0029907227 to 0.29882812
Outputs:
- cov_left_out: float32 [12, 128, 256, 256], P('grp', 'fsdp')
- cov_right_out: float32 [12, 128, 256, 256], P('grp', 'fsdp')
- first_out: bfloat16 [12, 128, 256, 256], P('grp', 'fsdp')
- second_out: bfloat16 [12, 128, 256, 256], P('grp', 'fsdp')
- flat_update: bfloat16 [12, 32768, 256], P('grp', 'fsdp')
Inputs may be any that keep to these rules, and one draw needn't show every extreme that they name: `row_block`: in each group every (block, row) pair appears exactly once. Each device's flat rows are intervals of 8 consecutive rows of one block; from one device exactly 8 rows go to the blocks of each fsdp index (owner of a block = block_home // 2). `block_home`: each group's row is a permutation of 0 to 127; state index h lies on fsdp index h // 2.
All inputs are finite; a program needn't handle non-finite values.
Results may differ from a plain program's by a relative error of at most 0.0025.
The roundings to bfloat16 on the way count: a program that leaves them out, or rounds other values in their place, can miss the bound.
Values may be sent and summed in bfloat16 or wider, within the bound.
A program may use at most 32 MiB of HBM per device.

v0:
```python
import jax
import jax.numpy as jnp
from jax import lax
from jax.sharding import Mesh
from jax.sharding import PartitionSpec as P

FSDP = ("fsdp_0", "fsdp_1", "fsdp_2")
FSDP_GRP = ("fsdp_0", "fsdp_1", "fsdp_2", "grp")


clip_rms = 0.25
beta_cov = 0.95
beta_first = 0.95
beta_second = 0.95
epsilon = 1e-08


def over_axes(shard, axes):
    for axis in axes:
        shard = lax.psum(shard, axis)
    return shard


def send_owners(outgoing, labels):
    return (
        lax.all_to_all(outgoing, FSDP, split_axis=0, concat_axis=0, tiled=True),
        lax.all_to_all(labels, FSDP, split_axis=0, concat_axis=0, tiled=True),
    )


def shards(
    grad_flat,
    row_block,
    row_index,
    block_home,
    cov_left,
    cov_right,
    basis_left,
    basis_right,
    moment_first,
    moment_second,
):
    devices = lax.axis_size(FSDP)
    row_count = grad_flat.shape[1]
    width = grad_flat.shape[2]
    block_count = block_home.shape[1]
    per_owner = cov_left.shape[1]
    capacity = row_count // devices
    grad_rows = grad_flat[0]
    matches = row_block[0][:, None] == jnp.arange(block_count, dtype=jnp.int32)[None, :]
    home_slot = jnp.sum(jnp.where(matches, block_home[0][None, :], 0), axis=1)
    owner_index = home_slot // per_owner
    local_row = home_slot % per_owner * width + row_index[0]
    owner_hits = (owner_index[:, None] == jnp.arange(devices, dtype=jnp.int32)[None, :]).astype(
        jnp.int32
    )
    earlier = jnp.cumsum(owner_hits, axis=0) - owner_hits
    slot_number = jnp.sum(earlier * owner_hits, axis=1)
    position = owner_index * capacity + slot_number
    outgoing = jnp.zeros((devices * capacity, width), grad_rows.dtype).at[position].set(grad_rows)
    labels = jnp.full((devices * capacity,), -1, jnp.int32).at[position].set(local_row)
    outgoing = outgoing.reshape(devices, capacity, width)
    labels = labels.reshape(devices, capacity)
    grad_wide = grad_rows.astype(jnp.float32)
    sum_squares = over_axes(jnp.sum(grad_wide * grad_wide), FSDP_GRP)
    arrived, arrived_labels = send_owners(outgoing, labels)
    arrived_labels = arrived_labels.reshape(-1)
    target = jnp.where(arrived_labels >= 0, arrived_labels, row_count)
    stacked = (
        jnp.zeros((row_count, width), grad_rows.dtype)
        .at[target]
        .set(arrived.reshape(-1, width), mode="drop")
    )
    blocks = stacked.reshape(per_owner, width, width)
    entries = devices * lax.axis_size("grp") * row_count * width
    root_mean = jnp.sqrt(sum_squares / entries + 1e-06)
    clip_scale = jnp.minimum(1.0, clip_rms / root_mean)
    clipped = (clip_scale * blocks.astype(jnp.float32)).astype(jnp.bfloat16)
    left_new = beta_cov * cov_left[0] + (1.0 - beta_cov) * jnp.einsum(
        "kij,klj->kil", clipped, clipped, preferred_element_type=jnp.float32
    )
    right_new = beta_cov * cov_right[0] + (1.0 - beta_cov) * jnp.einsum(
        "kji,kjl->kil", clipped, clipped, preferred_element_type=jnp.float32
    )
    basis_l = basis_left[0]
    basis_r = basis_right[0]
    turned = jnp.einsum(
        "kji,kjl->kil", basis_l, clipped, preferred_element_type=jnp.float32
    ).astype(jnp.bfloat16)
    rotated = jnp.einsum("kij,kjl->kil", turned, basis_r, preferred_element_type=jnp.float32)
    first_new = beta_first * moment_first[0].astype(jnp.float32) + (1.0 - beta_first) * rotated
    second_new = (
        beta_second * moment_second[0].astype(jnp.float32) + (1.0 - beta_second) * rotated * rotated
    )
    normalized = (first_new / (jnp.sqrt(second_new) + epsilon)).astype(jnp.bfloat16)
    back_left = jnp.einsum(
        "kij,kjl->kil", basis_l, normalized, preferred_element_type=jnp.float32
    ).astype(jnp.bfloat16)
    pick_rows = jnp.maximum(arrived_labels, 0)
    update = jnp.einsum(
        "kij,klj->kil", back_left, basis_r, preferred_element_type=jnp.float32
    ).astype(jnp.bfloat16)
    part_width = update.shape[2]
    chosen = update.reshape(row_count, part_width)[pick_rows]
    returned = lax.all_to_all(
        chosen.reshape(devices, capacity, part_width), FSDP, split_axis=0, concat_axis=0, tiled=True
    )
    flat_rows = returned.reshape(devices * capacity, width)[position]
    return (
        left_new[None],
        right_new[None],
        first_new.astype(jnp.bfloat16)[None],
        second_new.astype(jnp.bfloat16)[None],
        flat_rows[None],
    )


def solution(mesh):
    split = Mesh(
        mesh.devices.reshape(4, 8, 2, mesh.shape["grp"]), ("fsdp_0", "fsdp_1", "fsdp_2", "grp")
    )
    return jax.shard_map(
        shards,
        mesh=split,
        in_specs=(
            P("grp", FSDP, None),
            P("grp", FSDP),
            P("grp", FSDP),
            P("grp", None),
            P("grp", FSDP, None, None),
            P("grp", FSDP, None, None),
            P("grp", FSDP, None, None),
            P("grp", FSDP, None, None),
            P("grp", FSDP, None, None),
            P("grp", FSDP, None, None),
        ),
        out_specs=(
            P("grp", FSDP, None, None),
            P("grp", FSDP, None, None),
            P("grp", FSDP, None, None),
            P("grp", FSDP, None, None),
            P("grp", FSDP, None),
        ),
        check_vma=False,
    )
```

profile of v0, /device:TPU:1, one launch (start us, length us, event | category | flops | bytes accessed | tf_op | source)
XLA Modules:
  0.0 129.7 jit_solution(12792966210233846981)
XLA Ops:
  0.7 0.7 copy-done.7
  1.4 0.2 select_reduce_fusion
  1.6 0.7 copy-done.8
  2.3 1.2 reduce-window.6
  3.5 0.2 slice_reduce_fusion
  3.8 0.1 fusion.22
  4.0 2.4 %scatter_custom_fusion = s32[512]{0:T(512)S(1)} fusion(s32[512]{0:T(512)S(1)} %bitcast.117, s32[512]{0:T(512)S(1)} %get-tuple-element.9, s32[]{:T(128)} %constant.51.clone.1), kind=kCustom, calls=%fused_computation.75 | custom fusion | bytes 2052 | tf_op jit(solution)/shard_map/scatter | solution.py:61
  6.4 0.7 all_to_all.12
  7.1 14.5 %all-to-all-start = ((s32[64,1,8]{2,1,0:T(1,128)}), s32[64,1,8]{2,1,0:T(1,128)S(1)}, u32[]{:S(2)}, u32[]{:S(2)}) async-start(s32[64,1,8]{2,1,0:T(1,128)} %bitcast.10), calls=%async_computation | async-start | bytes 65536 | tf_op jit(solution)/shard_map/all_to_all | solution.py:27
  21.6 3.0 %scatter_custom_fusion.1 = bf16[512,256]{1,0:T(8,128)(2,1)} fusion(s32[512]{0:T(512)S(1)} %bitcast.118, bf16[1,512,256]{2,1,0:T(8,128)(2,1)S(1)} %copy-done.1, bf16[]{:T(256)} %constant.50.clone.1), kind=kCustom, calls=%fused_computation.31 | custom fusion | bytes 524290 | tf_op jit(solution)/shard_map/scatter | solution.py:60
  24.6 6.4 %all-to-all-done = s32[64,1,8]{2,1,0:T(1,128)S(1)} async-done(((s32[64,1,8]{2,1,0:T(1,128)}), s32[64,1,8]{2,1,0:T(1,128)S(1)}, u32[]{:S(2)}, u32[]{:S(2)}) %all-to-all-start) | async-done | bytes 2080 | tf_op jit(solution)/shard_map/all_to_all | solution.py:27
  31.0 4.7 %all-to-all-start.1 = ((bf16[64,8,256]{2,1,0:T(8,128)(2,1)}), bf16[64,8,256]{2,1,0:T(8,128)(2,1)S(1)}, u32[]{:S(2)}, u32[]{:S(2)}) async-start(bf16[64,8,256]{2,1,0:T(8,128)(2,1)} %bitcast.12), calls=%async_computation.1 | async-start | bytes 524288 | tf_op jit(solution)/shard_map/all_to_all | solution.py:26
  35.7 0.7 multiply_reduce_fusion
  36.4 10.2 %psum.28 = f32[]{:T(128)} all-reduce(f32[]{:T(128)} %multiply_reduce_fusion), channel_id=1, replica_groups=mesh['fsdp_0'=4,'fsdp_1'=8,'fsdp_2'=2,'grp'=12] {'fsdp_0'}, use_global_device_ids=true, to_apply=%region_1.2 | all-reduce | flops 1 | bytes 8 | tf_op jit(solution)/shard_map/psum | solution.py:20
  46.7 13.7 %psum.29 = f32[]{:T(128)} all-reduce(f32[]{:T(128)} %psum.28), channel_id=1, replica_groups=mesh['fsdp_0'=4,'fsdp_1'=8,'fsdp_2'=2,'grp'=12] {'fsdp_1'}, use_global_device_ids=true, to_apply=%region_2.3 | all-reduce | flops 1 | bytes 8 | tf_op jit(solution)/shard_map/psum | solution.py:20
  60.4 8.2 %psum.30 = f32[]{:T(128)} all-reduce(f32[]{:T(128)} %psum.29), channel_id=1, replica_groups=mesh['fsdp_0'=4,'fsdp_1'=8,'fsdp_2'=2,'grp'=12] {'fsdp_2'}, use_global_device_ids=true, to_apply=%region_3.4 | all-reduce | flops 1 | bytes 8 | tf_op jit(solution)/shard_map/psum | solution.py:20
  68.6 25.7 %psum.31 = f32[]{:T(128)} all-reduce(f32[]{:T(128)} %psum.30), channel_id=1, replica_groups=mesh['fsdp_0'=4,'fsdp_1'=8,'fsdp_2'=2,'grp'=12] {'grp'}, use_global_device_ids=true, to_apply=%region_4.5 | all-reduce | flops 1 | bytes 8 | tf_op jit(solution)/shard_map/psum | solution.py:20
  95.0 0.5 broadcast.234
  95.5 0.7 reduce.5
  96.3 0.1 reshape.176
  96.4 2.4 %scatter_custom_fusion.2 = bf16[512,256]{1,0:T(8,128)(2,1)S(1)} fusion(s32[512]{0:T(512)S(1)} %bitcast.121, bf16[64,8,256]{2,1,0:T(8,128)(2,1)S(1)} %all-to-all-done.1, bf16[]{:T(256)} %constant.50.clone.1), kind=kCustom, calls=%fused_computation.29 | custom fusion | bytes 524290 | tf_op jit(solution)/shard_map/scatter | solution.py:72
  98.9 0.9 copy-done.4
  99.8 0.5 fusion.4
  100.3 0.4 copy-done.5
  100.8 0.8 convolution_convert_fusion
  101.5 2.6 %gather_fusion = bf16[512,256]{1,0:T(8,128)(2,1)} fusion(bf16[512,256]{1,0:T(8,128)(2,1)S(1)} %bitcast.110, s32[1024]{0:T(1024)S(1)} %pad_clamp_fusion.1), kind=kCustom, calls=%fused_computation | custom fusion | bytes 526336 | tf_op jit(solution)/shard_map/gather | solution.py:104
  104.1 11.0 %all-to-all-start.2 = ((bf16[64,8,256]{2,1,0:T(8,128)(2,1)}), bf16[64,8,256]{2,1,0:T(8,128)(2,1)S(1)}, u32[]{:S(2)}, u32[]{:S(2)}) async-start(bf16[64,8,256]{2,1,0:T(8,128)(2,1)} %bitcast.26), calls=%async_computation.2 | async-start | bytes 524288 | tf_op jit(solution)/shard_map/all_to_all | solution.py:105
  115.2 1.1 fusion.1
  116.3 1.1 fusion.3
  117.3 0.9 fusion.8
  118.3 8.9 %all-to-all-done.2 = bf16[64,8,256]{2,1,0:T(8,128)(2,1)S(1)} async-done(((bf16[64,8,256]{2,1,0:T(8,128)(2,1)}), bf16[64,8,256]{2,1,0:T(8,128)(2,1)S(1)}, u32[]{:S(2)}, u32[]{:S(2)}) %all-to-all-start.2) | async-done | bytes 262176 | tf_op jit(solution)/shard_map/all_to_all | solution.py:105
  127.1 2.6 %gather_fusion.1 = bf16[512,256]{1,0:T(8,128)(2,1)} fusion(bf16[512,256]{1,0:T(8,128)(2,1)S(1)} %bitcast.109, s32[1024]{0:T(1024)S(1)} %pad_clamp_fusion), kind=kCustom, calls=%fused_computation.1 | custom fusion | bytes 526336 | tf_op jit(solution)/shard_map/gather | solution.py:108
  (27 shorter events, 0.3 us)
Async XLA Ops:
  0.6 98.2 %copy-start = (bf16[1,2,256,256]{3,2,1,0:T(8,128)(2,1)S(1)}, bf16[1,2,256,256]{3,2,1,0:T(8,128)(2,1)}, u32[]{:S(2)}) copy-start(bf16[1,2,256,256]{3,2,1,0:T(8,128)(2,1)} %param.17) | copy-start | bytes 786436
  0.6 0.7 copy-start.7
  0.7 0.7 copy-start.9
  1.6 0.7 copy-start.8
  3.5 18.1 %copy-start.1 = (bf16[1,512,256]{2,1,0:T(8,128)(2,1)S(1)}, bf16[1,512,256]{2,1,0:T(8,128)(2,1)}, u32[]{:S(2)}) copy-start(bf16[1,512,256]{2,1,0:T(8,128)(2,1)} %param.10) | copy-start | bytes 786436
  7.1 23.9 %all-to-all-start = ((s32[64,1,8]{2,1,0:T(1,128)}), s32[64,1,8]{2,1,0:T(1,128)S(1)}, u32[]{:S(2)}, u32[]{:S(2)}) async-start(s32[64,1,8]{2,1,0:T(1,128)} %bitcast.10), calls=%async_computation | async-start | bytes 65536 | tf_op jit(solution)/shard_map/all_to_all | solution.py:27
  31.0 65.4 %all-to-all-start.1 = ((bf16[64,8,256]{2,1,0:T(8,128)(2,1)}), bf16[64,8,256]{2,1,0:T(8,128)(2,1)S(1)}, u32[]{:S(2)}, u32[]{:S(2)}) async-start(bf16[64,8,256]{2,1,0:T(8,128)(2,1)} %bitcast.12), calls=%async_computation.1 | async-start | bytes 524288 | tf_op jit(solution)/shard_map/all_to_all | solution.py:26
  98.8 1.0 copy-start.4
  99.8 0.9 copy-start.5
  99.8 1.0 copy-start.6
  104.1 11.0 %copy-start.2 = (f32[1,2,256,256]{3,2,1,0:T(8,128)S(1)}, f32[1,2,256,256]{3,2,1,0:T(8,128)}, u32[]{:S(2)}) copy-start(f32[1,2,256,256]{3,2,1,0:T(8,128)} %param.15) | copy-start | bytes 1572868
  104.1 23.0 %all-to-all-start.2 = ((bf16[64,8,256]{2,1,0:T(8,128)(2,1)}), bf16[64,8,256]{2,1,0:T(8,128)(2,1)S(1)}, u32[]{:S(2)}, u32[]{:S(2)}) async-start(bf16[64,8,256]{2,1,0:T(8,128)(2,1)} %bitcast.26), calls=%async_computation.2 | async-start | bytes 524288 | tf_op jit(solution)/shard_map/all_to_all | solution.py:105
  115.2 1.1 copy-start.3
where the time goes:
time: 130 us
  blocking collectives  57.9 us (45%)
  starting transfers between devices  30.2 us (23%)
  local copies, waits for them, and re-layouts  17.3 us (13%)
  waiting for transfers between devices  15.2 us (12%)
  other arithmetic  4.13 us (3%)
  matrix products  3.42 us (3%)
  between operations  1.53 us (1%)
    psum x4, blocking collectives, over_axes(): shard = lax.psum(shard, axis)  57.9 us
    all_to_all x1, starting transfers between devices, send_owners(): lax.all_to_all(labels, FSDP, split_axis=0, concat_axis=0, tiled=True)  14.5 us
    all_to_all x1, starting transfers between devices, shards(): lax.all_to_all(chosen.reshape(devices, capacity, part_width), FSDP, split...  11 us
    all_to_all x1, waiting for transfers between devices, shards(): lax.all_to_all(chosen.reshape(devices, capacity, part_width), FSDP, split...  8.85 us
    all_to_all x1, waiting for transfers between devices, send_owners(): lax.all_to_all(labels, FSDP, split_axis=0, concat_axis=0, tiled=True)  6.35 us
    all_to_all x1, starting transfers between devices, send_owners(): lax.all_to_all(outgoing, FSDP, split_axis=0, concat_axis=0, tiled=True)  4.72 us
    scatter x1, local copies, waits for them, and re-layouts, shards(): jnp.zeros((devices * capacity, width), grad_rows.dtype).at[position]  2.99 us
    unnamed x20, local copies, waits for them, and re-layouts  2.79 us
  transfers between devices with their start and end apart: 3, of which 2 were waited for; matrix products, arithmetic and copies ran while one was open for 6% of the time, Pallas kernels for 0%

commit v1 on v0

v1 whole, which is shorter than its diff:
```python
import functools

import jax
import jax.numpy as jnp
from jax import lax
from jax.experimental import pallas as pl
from jax.experimental.pallas import tpu as pltpu
from jax.sharding import PartitionSpec as P

MESH = pl.DeviceIdType.MESH

CLIP_RMS = 0.25
BETA = 0.95
EPS = 1e-08
PIECE = 8
LANES = 128

STAGE = 9


def iota(shape, dim):
    return lax.broadcasted_iota(jnp.int32, shape, dim)


def hot(hits):
    return jnp.where(hits, 1.0, 0.0).astype(jnp.bfloat16)


def dot(a, b, dims=((1,), (0,))):
    return lax.dot_general(a, b, (dims, ((), ())), preferred_element_type=jnp.float32)


def kernel(
    entries,
    n,
    groups,
    grad_hbm,
    row_block_hbm,
    row_index_hbm,
    home_hbm,
    cov_l_hbm,
    cov_r_hbm,
    basis_l_hbm,
    basis_r_hbm,
    first_hbm,
    second_hbm,
    cov_l_out,
    cov_r_out,
    first_out,
    second_out,
    flat_out,
    grad_v,
    row_block_v,
    row_index_v,
    home_v,
    cov_l_v,
    cov_r_v,
    basis_l_v,
    basis_r_v,
    first_v,
    second_v,
    clipped_v,
    send_a,
    recv_a,
    send_b,
    recv_b,
    meta_out,
    meta_in,
    sum_out,
    sum_in,
    to_owner,
    from_owner,
    to_state,
    from_state,
    flat_v,
    in_sem,
    out_sem,
    send_sem,
    recv_sem,
):
    me = lax.axis_index("fsdp")
    mine = lax.axis_index("grp")
    rows, width = grad_v.shape
    blocks = home_v.shape[1]
    per_owner = cov_l_v.shape[0]
    per_block = width // PIECE

    barrier = pltpu.get_barrier_semaphore()

    def peer(k):
        return lax.rem(me + k, n)

    def mate(k):
        return lax.rem(mine + k, groups)

    def greet(k, carry):
        pl.semaphore_signal(barrier, inc=1, device_id=(peer(k), mine), device_id_type=MESH)
        return carry

    def greet_mate(k, carry):
        pl.semaphore_signal(barrier, inc=1, device_id=(me, mate(k)), device_id_type=MESH)
        return carry

    lax.fori_loop(1, n, greet, 0)
    lax.fori_loop(1, groups, greet_mate, 0)

    loads = [
        pltpu.make_async_copy(source, target, in_sem.at[i])
        for i, (source, target) in enumerate(
            [
                (row_block_hbm, row_block_v),
                (home_hbm, home_v),
                (row_index_hbm, row_index_v),
                (grad_hbm.at[0], grad_v),
                (basis_l_hbm.at[0], basis_l_v),
                (basis_r_hbm.at[0], basis_r_v),
                (first_hbm.at[0], first_v),
                (second_hbm.at[0], second_v),
                (cov_l_hbm.at[0], cov_l_v),
                (cov_r_hbm.at[0], cov_r_v),
            ]
        )
    ]
    for load in loads:
        load.start()
    for load in loads[:3]:
        load.wait()

    lookup = hot(iota((blocks, rows), 0) == row_block_v[...])
    homes = jnp.broadcast_to(home_v[...].astype(jnp.float32), (8, blocks)).astype(jnp.bfloat16)
    home = dot(homes, lookup)[0:1].astype(jnp.int32)
    owner = home // per_owner
    piece = (home % per_owner) * per_block + row_index_v[...] // PIECE
    inner = iota((1, rows), 1) % PIECE
    to_owner[...] = hot(iota((rows, rows), 0) == owner * PIECE + inner)
    label = jnp.sum(
        jnp.where(iota((n, rows), 0) == owner, piece.astype(jnp.float32), 0.0), axis=1, keepdims=True
    ) * (1.0 / PIECE)
    meta_out[:, 0, :] = jnp.broadcast_to(label, (n, LANES))

    loads[3].wait()
    grad = grad_v[...]
    wide = grad.astype(jnp.float32)
    total = jnp.sum(jnp.sum(wide * wide, axis=0, keepdims=True), axis=1, keepdims=True)
    meta_out[:, 1, :] = jnp.broadcast_to(total, (n, LANES))
    send_a[...] = dot(to_owner[...], grad).reshape(n, PIECE, width).astype(jnp.bfloat16)

    pl.semaphore_wait(barrier, n - 1 + groups - 1)

    def send_meta(k, carry):
        pltpu.make_async_remote_copy(
            meta_out.at[peer(k)], meta_in.at[me], send_sem.at[0], recv_sem.at[0],
            device_id=(peer(k), mine), device_id_type=MESH,
        ).start()
        return carry

    def send_rows(k, carry):
        pltpu.make_async_remote_copy(
            send_a.at[peer(k)], recv_a.at[me], send_sem.at[1], recv_sem.at[1],
            device_id=(peer(k), mine), device_id_type=MESH,
        ).start()
        return carry

    def send_sum(k, carry):
        pltpu.make_async_remote_copy(
            sum_out, sum_in.at[mine], send_sem.at[2], recv_sem.at[2],
            device_id=(me, mate(k)), device_id_type=MESH,
        ).start()
        return carry

    def send_update(k, carry):
        pltpu.make_async_remote_copy(
            send_b.at[peer(k)], recv_b.at[me], send_sem.at[3], recv_sem.at[3],
            device_id=(peer(k), mine), device_id_type=MESH,
        ).start()
        return carry

    def wait_for(buffer, count, sem):
        part = buffer.at[pl.ds(0, count)]
        pltpu.make_async_copy(part, part, sem).wait()

    lax.fori_loop(1, n, send_meta, 0)
    lax.fori_loop(1, n, send_rows, 0)
    meta_in[me] = meta_out[me]
    recv_a[me] = send_a[me]

    spread = dot(
        jnp.broadcast_to(owner.astype(jnp.float32), (8, rows)).astype(jnp.bfloat16),
        jnp.ones((8, LANES), jnp.bfloat16),
        ((0,), (0,)),
    )
    place = spread.astype(jnp.int32) + iota((rows, LANES), 0) % PIECE
    for c in range(rows // LANES):
        from_owner[:, c * LANES : (c + 1) * LANES] = hot(iota((rows, LANES), 1) + c * LANES == place)

    wait_for(meta_in, n - 1, recv_sem.at[0])
    sum_out[...] = jnp.sum(meta_in[:, 1, :], axis=0, keepdims=True)
    lax.fori_loop(1, groups, send_sum, 0)
    sum_in[mine] = sum_out[...]

    came = meta_in[:, 0, :]
    came_column = jnp.broadcast_to(meta_in[:, 0:1, :], (n, PIECE, LANES)).reshape(rows, LANES)
    place = came_column.astype(jnp.int32) * PIECE + iota((rows, LANES), 0) % PIECE
    for c in range(rows // LANES):
        to_state_c = hot(iota((rows, LANES), 1) + c * LANES == place)
        from_state[:, c * LANES : (c + 1) * LANES] = to_state_c
    came_row = dot(
        came.astype(jnp.bfloat16), hot(iota((n, rows), 0) == iota((n, rows), 1) // PIECE), ((0,), (0,))
    )[0:1].astype(jnp.int32)
    to_state[...] = hot(iota((rows, rows), 0) == came_row * PIECE + inner)

    for load in loads[4:]:
        load.wait()
    wait_for(recv_a, n - 1, recv_sem.at[1])
    arrived = recv_a[...].astype(jnp.float32).reshape(rows, width).astype(jnp.bfloat16)
    stacked = dot(to_state[...], arrived)

    wait_for(sum_in, groups - 1, recv_sem.at[2])
    sum_squares = jnp.sum(sum_in[:, 0, :], axis=0, keepdims=True)
    scale = jnp.minimum(1.0, CLIP_RMS / jnp.sqrt(sum_squares / entries + 1e-06))[:, 0:1]
    clipped = (scale * stacked).astype(jnp.bfloat16)
    clipped_v[...] = clipped.reshape(per_owner, width, width)

    updates = []
    for b in range(per_owner):
        basis_l = basis_l_v[b]
        basis_r = basis_r_v[b]
        block = clipped[b * width : (b + 1) * width]
        turned = dot(basis_l, block, ((0,), (0,))).astype(jnp.bfloat16)
        rotated = dot(turned, basis_r)
        m = BETA * first_v[b].astype(jnp.float32) + (1.0 - BETA) * rotated
        v = BETA * second_v[b].astype(jnp.float32) + (1.0 - BETA) * rotated * rotated
        first_v[b] = m.astype(jnp.bfloat16)
        second_v[b] = v.astype(jnp.bfloat16)
        normalized = (m / (jnp.sqrt(v) + EPS)).astype(jnp.bfloat16)
        back = dot(basis_l, normalized).astype(jnp.bfloat16)
        updates.append(dot(back, basis_r, ((1,), (1,))).astype(jnp.bfloat16))
    update = jnp.concatenate(updates, axis=0)
    send_b[...] = dot(from_state[...], update).reshape(n, PIECE, width).astype(jnp.bfloat16)
    lax.fori_loop(1, n, send_update, 0)
    recv_b[me] = send_b[me]

    stores = [
        pltpu.make_async_copy(source, target, out_sem.at[i])
        for i, (source, target) in enumerate(
            [
                (first_v, first_out.at[0]),
                (second_v, second_out.at[0]),
                (cov_l_v, cov_l_out.at[0]),
                (cov_r_v, cov_r_out.at[0]),
                (flat_v, flat_out.at[0]),
            ]
        )
    ]
    stores[0].start()
    stores[1].start()
    for b in range(per_owner):
        block = clipped_v[b]
        cov_l_v[b] = BETA * cov_l_v[b] + (1.0 - BETA) * dot(block, block, ((1,), (1,)))
    stores[2].start()
    for b in range(per_owner):
        block = clipped_v[b]
        cov_r_v[b] = BETA * cov_r_v[b] + (1.0 - BETA) * dot(block, block, ((0,), (0,)))
    stores[3].start()

    wait_for(recv_b, n - 1, recv_sem.at[3])
    returned = recv_b[...].astype(jnp.float32).reshape(rows, width).astype(jnp.bfloat16)
    flat_v[...] = dot(from_owner[...], returned).astype(jnp.bfloat16)
    stores[4].start()

    wait_for(meta_out, n - 1, send_sem.at[0])
    wait_for(send_a, n - 1, send_sem.at[1])
    wait_for(sum_in, groups - 1, send_sem.at[2])
    wait_for(send_b, n - 1, send_sem.at[3])
    for store in stores:
        store.wait()


def solution(mesh):
    n = mesh.shape["fsdp"]
    groups = mesh.shape["grp"]

    def shard(grad, row_block, row_index, home, cov_l, cov_r, basis_l, basis_r, first, second):
        rows, width = grad.shape[1:]
        per_owner = cov_l.shape[1]
        block = (per_owner, width, width)
        f32, bf16, i32 = jnp.float32, jnp.bfloat16, jnp.int32
        vmem = pltpu.VMEM
        anywhere = pl.BlockSpec(memory_space=pl.ANY)
        entries = float(n * groups * rows * width)
        return pl.pallas_call(
            functools.partial(kernel, entries, n, groups),
            out_shape=(
                jax.ShapeDtypeStruct(cov_l.shape, f32),
                jax.ShapeDtypeStruct(cov_r.shape, f32),
                jax.ShapeDtypeStruct(first.shape, bf16),
                jax.ShapeDtypeStruct(second.shape, bf16),
                jax.ShapeDtypeStruct(grad.shape, bf16),
            ),
            in_specs=[anywhere] * 10,
            out_specs=(anywhere,) * 5,
            scratch_shapes=[
                vmem((rows, width), bf16),
                vmem(row_block.shape, i32),
                vmem(row_index.shape, i32),
                vmem(home.shape, i32),
                vmem(block, f32),
                vmem(block, f32),
                vmem(block, bf16),
                vmem(block, bf16),
                vmem(block, bf16),
                vmem(block, bf16),
                vmem(block, bf16),
                vmem((n, PIECE, width), bf16),
                vmem((n, PIECE, width), bf16),
                vmem((n, PIECE, width), bf16),
                vmem((n, PIECE, width), bf16),
                vmem((n, 2, LANES), f32),
                vmem((n, 2, LANES), f32),
                vmem((1, LANES), f32),
                vmem((groups, 1, LANES), f32),
                vmem((rows, rows), bf16),
                vmem((rows, rows), bf16),
                vmem((rows, rows), bf16),
                vmem((rows, rows), bf16),
                vmem((rows, width), bf16),
                pltpu.SemaphoreType.DMA((10,)),
                pltpu.SemaphoreType.DMA((5,)),
                pltpu.SemaphoreType.DMA((4,)),
                pltpu.SemaphoreType.DMA((4,)),
            ],
            compiler_params=pltpu.CompilerParams(collective_id=0, has_side_effects=True),
            name="soap_step",
        )(grad, row_block, row_index, home, cov_l, cov_r, basis_l, basis_r, first, second)

    flat = P("grp", "fsdp", None)
    index = P("grp", "fsdp")
    state = P("grp", "fsdp", None, None)
    return jax.shard_map(
        shard,
        mesh=mesh,
        in_specs=(flat, index, index, P("grp", None)) + (state,) * 6,
        out_specs=(state,) * 4 + (flat,),
        check_vma=False,
    )
```

time: 130 us -> 50.4 us (0.39)
  blocking collectives: 57.9 us -> 0 us
  Pallas kernels: 0 us -> 43.6 us
  starting transfers between devices: 30.2 us -> 0 us
  waiting for transfers between devices: 15.2 us -> 0 us
  local copies, waits for them, and re-layouts: 17.3 us -> 5.81 us
  other arithmetic: 4.13 us -> 0 us
  matrix products: 3.42 us -> 0 us
    psum x4 -> x0, blocking collectives: 57.9 us -> none  [over_axes(): shard = lax.psum(shard, axis)]
    pallas_call x0 -> x1, Pallas kernels: none -> 43.6 us  [shard(): pl.pallas_call(functools.partial(kernel, entries, n, groups), out_shape=(...]
    all_to_all x3 -> x0, starting transfers between devices: 30.2 us -> none  [the longest x1 14.5 us: send_owners(): lax.all_to_all(labels, FSDP, split_axis=0, concat_axis=0, tiled=True)]
    all_to_all x3 -> x0, waiting for transfers between devices: 15.2 us -> none  [the longest x1 8.85 us: shards(): lax.all_to_all(chosen.reshape(devices, capacity, part_width), FSDP, split...]
    scatter x3 -> x0, local copies, waits for them, and re-layouts: 7.81 us -> none  [the longest x1 2.99 us: shards(): jnp.zeros((devices * capacity, width), grad_rows.dtype).at[position]]
    gather x2 -> x0, local copies, waits for them, and re-layouts: 5.15 us -> none  [the longest x1 2.58 us: shards(): chosen = update.reshape(row_count, part_width)[pick_rows]]
    dot_general x4 -> x0, matrix products: 3.42 us -> none  [the longest x1 1.08 us: shards(): jnp.einsum('kji,kjl->kil', clipped, clipped, preferred_element_type=jnp.f...]
    unnamed x20 -> x13, local copies, waits for them, and re-layouts: 2.79 us -> 5.81 us
  transfers between devices with their start and end apart: 3 -> 0, of which waited for: 2 -> 0; matrix products, arithmetic and copies ran while one was open for 6% -> 0% of each run, Pallas kernels for 0% -> 0%
where the time goes in v1:
time: 50.4 us; the launch traced here: 50.1 us
  Pallas kernels  43.6 us (87%)
  local copies, waits for them, and re-layouts  5.81 us (12%)
  between operations  0.66 us (1%)
    pallas_call x1, Pallas kernels, shard(): pl.pallas_call(functools.partial(kernel, entries, n, groups), out_shape=(...  43.6 us
    unnamed x13, local copies, waits for them, and re-layouts  5.81 us

profile of v1, /device:TPU:1, one launch (start us, length us, event | category | flops | bytes accessed | tf_op | source)
XLA Modules:
  0.0 50.1 jit_solution(4477868987252341971)
XLA Ops:
  0.6 43.6 %soap_step.1 = (f32[1,2,256,256]{3,2,1,0:T(8,128)}, f32[1,2,256,256]{3,2,1,0:T(8,128)}, bf16[1,2,256,256]{3,2,1,0:T(8,128)(2,1)}, bf16[1,2,256,256]{3,2,1,0:T(8,128)(2,1)}, bf16[1,512,256]{2,1,0:T(8,128)(2,1)}) custom-call(bf16[1,512,256]{2,1,0:T(8,128)(2,1)} %grad_hbm.1, s32[1,512]{1,0:T(1,128)} %row_block_hbm.1, s32[1,512]{1,0:T(1,128)} %row_index_hbm.1, ...), custom_call_target="tpu_custom_call" | custom-call | tf_op jit(solution)/shard_map/soap_step/pallas_call | solution.py:291
  44.3 0.0 copy-start
  44.3 1.9 %copy.20 = f32[1,2,256,256]{3,2,1,0:T(8,128)} copy(f32[1,2,256,256]{3,2,1,0:T(8,128)} %get-tuple-element.10) | data formatting | bytes 1048576
  46.2 0.0 copy-done
  46.2 0.0 copy-start.3
  46.2 0.8 %copy.21 = f32[1,2,256,256]{3,2,1,0:T(8,128)} copy(f32[1,2,256,256]{3,2,1,0:T(8,128)S(1)} %copy-done) | data formatting | bytes 1048576
  47.0 0.3 copy-done.3
  47.3 0.0 copy-start.2
  47.3 0.7 %copy.22 = bf16[1,2,256,256]{3,2,1,0:T(8,128)(2,1)} copy(bf16[1,2,256,256]{3,2,1,0:T(8,128)(2,1)S(1)} %copy-done.3) | data formatting | bytes 524288
  48.0 0.3 copy-done.2
  48.3 0.0 copy-start.1
  48.3 0.7 %copy.23 = bf16[1,2,256,256]{3,2,1,0:T(8,128)(2,1)} copy(bf16[1,2,256,256]{3,2,1,0:T(8,128)(2,1)S(1)} %copy-done.2) | data formatting | bytes 524288
  49.0 0.3 copy-done.1
  49.4 0.7 %copy.24 = bf16[1,512,256]{2,1,0:T(8,128)(2,1)} copy(bf16[1,512,256]{2,1,0:T(8,128)(2,1)S(1)} %copy-done.1) | data formatting | bytes 524288
Async XLA Ops:
  44.3 1.9 %copy-start = (f32[1,2,256,256]{3,2,1,0:T(8,128)S(1)}, f32[1,2,256,256]{3,2,1,0:T(8,128)}, u32[]{:S(2)}) copy-start(f32[1,2,256,256]{3,2,1,0:T(8,128)} %get-tuple-element.11) | copy-start | bytes 1572868
  46.2 1.1 %copy-start.3 = (bf16[1,2,256,256]{3,2,1,0:T(8,128)(2,1)S(1)}, bf16[1,2,256,256]{3,2,1,0:T(8,128)(2,1)}, u32[]{:S(2)}) copy-start(bf16[1,2,256,256]{3,2,1,0:T(8,128)(2,1)} %get-tuple-element.12) | copy-start | bytes 786436
  47.3 1.0 %copy-start.2 = (bf16[1,2,256,256]{3,2,1,0:T(8,128)(2,1)S(1)}, bf16[1,2,256,256]{3,2,1,0:T(8,128)(2,1)}, u32[]{:S(2)}) copy-start(bf16[1,2,256,256]{3,2,1,0:T(8,128)(2,1)} %get-tuple-element.13) | copy-start | bytes 786436
  48.3 1.0 %copy-start.1 = (bf16[1,512,256]{2,1,0:T(8,128)(2,1)S(1)}, bf16[1,512,256]{2,1,0:T(8,128)(2,1)}, u32[]{:S(2)}) copy-start(bf16[1,512,256]{2,1,0:T(8,128)(2,1)} %get-tuple-element.14) | copy-start | bytes 786436

commit v2 on v1

v2 whole, which is shorter than its diff:
```python
import functools

import jax
import jax.numpy as jnp
from jax import lax
from jax.experimental import pallas as pl
from jax.experimental.pallas import tpu as pltpu
from jax.sharding import PartitionSpec as P

MESH = pl.DeviceIdType.MESH

CLIP_RMS = 0.25
BETA = 0.95
EPS = 1e-08
PIECE = 8
LANES = 128


def iota(shape, dim):
    return lax.broadcasted_iota(jnp.int32, shape, dim)


def hot(hits):
    return jnp.where(hits, 1.0, 0.0).astype(jnp.bfloat16)


def dot(a, b, dims=((1,), (0,))):
    return lax.dot_general(a, b, (dims, ((), ())), preferred_element_type=jnp.float32)


def steps(sizes):
    nx, ny, nc = sizes
    near_y = sorted(range(ny), key=lambda d: -min(d, ny - d))
    near_x = sorted(range(nx), key=lambda d: -min(d, nx - d))
    return [(dx, dy, dc) for dy in near_y for dx in near_x for dc in range(nc) if dx or dy or dc]


def kernel(
    entries,
    sizes,
    groups,
    grad_hbm,
    row_block_hbm,
    row_index_hbm,
    home_hbm,
    cov_l_hbm,
    cov_r_hbm,
    basis_l_hbm,
    basis_r_hbm,
    first_hbm,
    second_hbm,
    cov_l_out,
    cov_r_out,
    first_out,
    second_out,
    flat_out,
    grad_v,
    row_block_v,
    row_index_v,
    home_v,
    cov_l_v,
    cov_r_v,
    basis_l_v,
    basis_r_v,
    basis_l_t,
    first_v,
    second_v,
    stacked_v,
    clipped_v,
    send_a,
    recv_a,
    send_b,
    recv_b,
    meta_out,
    meta_in,
    part_out,
    part_in,
    sum_out,
    sum_in,
    all_out,
    all_in,
    to_owner,
    from_owner,
    to_state,
    from_state,
    in_sem,
    send_sem,
    recv_sem,
):
    me = lax.axis_index("fsdp")
    mine = lax.axis_index("grp")
    nx, ny, nc = sizes
    n = nx * ny * nc
    rows, width = grad_v.shape
    blocks = home_v.shape[1]
    per_owner = cov_l_v.shape[0]
    per_block = width // PIECE
    my_x, my_y, my_c = me // (ny * nc), lax.rem(me // nc, ny), lax.rem(me, nc)

    def peer(step):
        dx, dy, dc = step
        x, y, c = lax.rem(my_x + dx, nx), lax.rem(my_y + dy, ny), lax.rem(my_c + dc, nc)
        return (x * ny + y) * nc + c

    loads = [
        pltpu.make_async_copy(source, target, in_sem.at[i])
        for i, (source, target) in enumerate(
            [
                (grad_hbm.at[0], grad_v),
                (row_block_hbm, row_block_v),
                (home_hbm, home_v),
                (row_index_hbm, row_index_v),
                (basis_l_hbm.at[0], basis_l_v),
                (basis_r_hbm.at[0], basis_r_v),
                (first_hbm.at[0], first_v),
                (second_hbm.at[0], second_v),
                (cov_l_hbm.at[0], cov_l_v),
                (cov_r_hbm.at[0], cov_r_v),
            ]
        )
    ]
    for load in loads:
        load.start()

    barrier = pltpu.get_barrier_semaphore()
    for step in steps(sizes):
        pl.semaphore_signal(barrier, inc=1, device_id=(peer(step), mine), device_id_type=MESH)

    @pl.when(mine == 0)
    def _():
        def greet(g, carry):
            pl.semaphore_signal(barrier, inc=1, device_id=(me, g), device_id_type=MESH)
            return carry

        lax.fori_loop(1, groups, greet, 0)

    def send(source, target, k, to):
        pltpu.make_async_remote_copy(
            source, target, send_sem.at[k], recv_sem.at[k], device_id=to, device_id_type=MESH
        ).start()

    def to_peers(source, target, k):
        for step in steps(sizes):
            to = peer(step)
            send(source.at[to], target.at[me], k, (to, mine))

    def wait_for(buffer, count, sem):
        part = buffer.at[pl.ds(0, count)]
        pltpu.make_async_copy(part, part, sem).wait()

    loads[0].wait()
    wide = grad_v[...].astype(jnp.float32)
    total = jnp.sum(jnp.sum(wide * wide, axis=0, keepdims=True), axis=1, keepdims=True)
    part_out[...] = jnp.broadcast_to(total, (1, LANES))

    @pl.when(mine == 0)
    def _():
        part_in[0] = part_out[...]
        pl.semaphore_wait(barrier, n - 1)

    @pl.when(mine != 0)
    def _():
        pl.semaphore_wait(barrier, n)
        send(part_out, part_in.at[mine], 0, (me, 0))

    for load in loads[1:4]:
        load.wait()
    lookup = hot(iota((blocks, rows), 0) == row_block_v[...])
    homes = jnp.broadcast_to(home_v[...].astype(jnp.float32), (8, blocks)).astype(jnp.bfloat16)
    home = dot(homes, lookup)[0:1].astype(jnp.int32)
    owner = home // per_owner
    piece = (home % per_owner) * per_block + row_index_v[...] // PIECE
    inner = iota((1, rows), 1) % PIECE
    label = jnp.sum(
        jnp.where(iota((n, rows), 0) == owner, piece.astype(jnp.float32), 0.0), axis=1, keepdims=True
    ) * (1.0 / PIECE)
    meta_out[:, 0, :] = jnp.broadcast_to(label, (n, LANES))
    to_owner[...] = hot(iota((rows, rows), 0) == owner * PIECE + inner)
    send_a[...] = dot(to_owner[...], grad_v[...]).reshape(n, PIECE, width).astype(jnp.bfloat16)

    to_peers(meta_out, meta_in, 1)
    to_peers(send_a, recv_a, 2)
    meta_in[me] = meta_out[me]
    recv_a[me] = send_a[me]

    spread = dot(
        jnp.broadcast_to(owner.astype(jnp.float32), (8, rows)).astype(jnp.bfloat16),
        jnp.ones((8, LANES), jnp.bfloat16),
        ((0,), (0,)),
    )
    place = spread.astype(jnp.int32) + iota((rows, LANES), 0) % PIECE
    for c in range(rows // LANES):
        from_owner[:, c * LANES : (c + 1) * LANES] = hot(iota((rows, LANES), 1) + c * LANES == place)
    for load in loads[4:]:
        load.wait()
    for b in range(per_owner):
        basis_l_t[b] = basis_l_v[b].T

    wait_for(meta_in, n - 1, recv_sem.at[1])
    came_column = jnp.broadcast_to(meta_in[...], (n, PIECE, LANES)).reshape(rows, LANES)
    place = came_column.astype(jnp.int32) * PIECE + iota((rows, LANES), 0) % PIECE
    for c in range(rows // LANES):
        from_state[:, c * LANES : (c + 1) * LANES] = hot(iota((rows, LANES), 1) + c * LANES == place)
    came_row = dot(
        meta_in[:, 0, :].astype(jnp.bfloat16),
        hot(iota((n, rows), 0) == iota((n, rows), 1) // PIECE),
        ((0,), (0,)),
    )[0:1].astype(jnp.int32)
    to_state[...] = hot(iota((rows, rows), 0) == came_row * PIECE + inner)

    @pl.when(mine == 0)
    def _():
        wait_for(part_in, groups - 1, recv_sem.at[0])
        sum_out[...] = jnp.sum(part_in[:, 0, :], axis=0, keepdims=True)
        for step in steps(sizes):
            to = peer(step)
            send(sum_out, sum_in.at[me], 3, (to, mine))
        sum_in[me] = sum_out[...]

    wait_for(recv_a, n - 1, recv_sem.at[2])
    arrived = recv_a[...].astype(jnp.float32).reshape(rows, width).astype(jnp.bfloat16)
    stacked_v[...] = dot(to_state[...], arrived)

    @pl.when(mine == 0)
    def _():
        wait_for(sum_in, n - 1, recv_sem.at[3])
        all_out[...] = jnp.sum(sum_in[:, 0, :], axis=0, keepdims=True)

        def tell(g, carry):
            send(all_out, all_in, 4, (me, g))
            return carry

        lax.fori_loop(1, groups, tell, 0)
        all_in[...] = all_out[...]

    @pl.when(mine != 0)
    def _():
        pltpu.make_async_copy(all_in, all_in, recv_sem.at[4]).wait()

    scale = jnp.minimum(1.0, CLIP_RMS / jnp.sqrt(all_in[...] / entries + 1e-06))[:, 0:1]

    updates = []
    for b in range(per_owner):
        basis_l = basis_l_v[b]
        basis_r = basis_r_v[b]
        block = (scale * stacked_v[b * width : (b + 1) * width]).astype(jnp.bfloat16)
        clipped_v[b] = block
        turned = dot(basis_l_t[b], block).astype(jnp.bfloat16)
        rotated = dot(turned, basis_r)
        m = BETA * first_v[b].astype(jnp.float32) + (1.0 - BETA) * rotated
        v = BETA * second_v[b].astype(jnp.float32) + (1.0 - BETA) * rotated * rotated
        first_out[b] = m.astype(jnp.bfloat16)
        second_out[b] = v.astype(jnp.bfloat16)
        normalized = (m / (jnp.sqrt(v) + EPS)).astype(jnp.bfloat16)
        back = dot(basis_l, normalized).astype(jnp.bfloat16)
        updates.append(dot(back, basis_r, ((1,), (1,))).astype(jnp.bfloat16))
    update = jnp.concatenate(updates, axis=0)
    send_b[...] = dot(from_state[...], update).reshape(n, PIECE, width).astype(jnp.bfloat16)
    to_peers(send_b, recv_b, 5)
    recv_b[me] = send_b[me]

    for b in range(per_owner):
        block = clipped_v[b]
        cov_l_out[b] = BETA * cov_l_v[b] + (1.0 - BETA) * dot(block, block, ((1,), (1,)))
        cov_r_out[b] = BETA * cov_r_v[b] + (1.0 - BETA) * dot(block, block, ((0,), (0,)))

    wait_for(meta_out, n - 1, send_sem.at[1])
    wait_for(send_a, n - 1, send_sem.at[2])

    @pl.when(mine == 0)
    def _():
        wait_for(sum_in, n - 1, send_sem.at[3])
        wait_for(part_in, groups - 1, send_sem.at[4])

    @pl.when(mine != 0)
    def _():
        pltpu.make_async_copy(part_out, part_out, send_sem.at[0]).wait()

    wait_for(send_b, n - 1, send_sem.at[5])
    wait_for(recv_b, n - 1, recv_sem.at[5])
    returned = recv_b[...].astype(jnp.float32).reshape(rows, width).astype(jnp.bfloat16)
    flat_out[...] = dot(from_owner[...], returned).astype(jnp.bfloat16)


def keep(*refs):
    half = (len(refs) - 1) // 2
    sources, targets, sem = refs[:half], refs[half : 2 * half], refs[-1]
    stores = [
        pltpu.make_async_copy(source, target.at[0], sem.at[i])
        for i, (source, target) in enumerate(zip(sources, targets))
    ]
    for store in stores:
        store.start()
    for store in stores:
        store.wait()


def solution(mesh):
    n = mesh.shape["fsdp"]
    groups = mesh.shape["grp"]
    sizes = (4, n // 8, 2)

    def shard(grad, row_block, row_index, home, cov_l, cov_r, basis_l, basis_r, first, second):
        rows, width = grad.shape[1:]
        per_owner = cov_l.shape[1]
        block = (per_owner, width, width)
        f32, bf16, i32 = jnp.float32, jnp.bfloat16, jnp.int32
        vmem = pltpu.VMEM
        anywhere = pl.BlockSpec(memory_space=pl.ANY)
        here = pl.BlockSpec(memory_space=pltpu.VMEM)
        entries = float(n * groups * rows * width)
        results = pl.pallas_call(
            functools.partial(kernel, entries, sizes, groups),
            out_shape=(
                jax.ShapeDtypeStruct(block, f32),
                jax.ShapeDtypeStruct(block, f32),
                jax.ShapeDtypeStruct(block, bf16),
                jax.ShapeDtypeStruct(block, bf16),
                jax.ShapeDtypeStruct((rows, width), bf16),
            ),
            in_specs=[pl.BlockSpec(memory_space=pltpu.HBM)] * 10,
            out_specs=(here,) * 5,
            scratch_shapes=[
                vmem((rows, width), bf16),
                vmem(row_block.shape, i32),
                vmem(row_index.shape, i32),
                vmem(home.shape, i32),
                vmem(block, f32),
                vmem(block, f32),
                vmem(block, bf16),
                vmem(block, bf16),
                vmem(block, bf16),
                vmem(block, bf16),
                vmem(block, bf16),
                vmem((rows, width), f32),
                vmem(block, bf16),
                vmem((n, PIECE, width), bf16),
                vmem((n, PIECE, width), bf16),
                vmem((n, PIECE, width), bf16),
                vmem((n, PIECE, width), bf16),
                vmem((n, 1, LANES), f32),
                vmem((n, 1, LANES), f32),
                vmem((1, LANES), f32),
                vmem((groups, 1, LANES), f32),
                vmem((1, LANES), f32),
                vmem((n, 1, LANES), f32),
                vmem((1, LANES), f32),
                vmem((1, LANES), f32),
                vmem((rows, rows), bf16),
                vmem((rows, rows), bf16),
                vmem((rows, rows), bf16),
                vmem((rows, rows), bf16),
                pltpu.SemaphoreType.DMA((10,)),
                pltpu.SemaphoreType.DMA((6,)),
                pltpu.SemaphoreType.DMA((6,)),
            ],
            compiler_params=pltpu.CompilerParams(
                collective_id=0, has_side_effects=True, vmem_limit_bytes=24 * 1024 * 1024
            ),
            name="soap_step",
        )(
            *(
                pltpu.with_memory_space_constraint(x, pltpu.HBM)
                for x in (grad, row_block, row_index, home, cov_l, cov_r, basis_l, basis_r, first, second)
            )
        )
        return pl.pallas_call(
            keep,
            out_shape=tuple(jax.ShapeDtypeStruct((1,) + r.shape, r.dtype) for r in results),
            in_specs=[here] * 5,
            out_specs=(anywhere,) * 5,
            scratch_shapes=[pltpu.SemaphoreType.DMA((5,))],
            compiler_params=pltpu.CompilerParams(vmem_limit_bytes=8 * 1024 * 1024),
            name="keep",
        )(*results)

    flat = P("grp", "fsdp", None)
    index = P("grp", "fsdp")
    state = P("grp", "fsdp", None, None)
    return jax.shard_map(
        shard,
        mesh=mesh,
        in_specs=(flat, index, index, P("grp", None)) + (state,) * 6,
        out_specs=(state,) * 4 + (flat,),
        check_vma=False,
    )
```

time: 50.4 us -> 43.1 us (0.86)
  local copies, waits for them, and re-layouts: 5.81 us -> 0 us
  Pallas kernels: 43.6 us -> 42.3 us
    unnamed x13 -> x0, local copies, waits for them, and re-layouts: 5.81 us -> none
    pallas_call x1 -> x2, Pallas kernels: 43.6 us -> 42.3 us  [the longest x1 41 us: shard(): pl.pallas_call(functools.partial(kernel, entries, sizes, groups), out_sha...]
where the time goes in v2:
time: 43.1 us; the launch traced here: 42.9 us
  Pallas kernels  42.3 us (98%)
  between operations  0.64 us (1%)
    pallas_call x1, Pallas kernels, shard(): pl.pallas_call(functools.partial(kernel, entries, sizes, groups), out_sha...  41 us
    pallas_call x1, Pallas kernels, shard(): pl.pallas_call(keep, out_shape=tuple((jax.ShapeDtypeStruct((1,) + r.shape...  1.27 us

profile of v2, /device:TPU:1, one launch (start us, length us, event | category | flops | bytes accessed | tf_op | source)
XLA Modules:
  0.0 42.9 jit_solution(4614401875948197579)
XLA Ops:
  0.6 41.0 %soap_step.1 = (f32[2,256,256]{2,1,0:T(8,128)S(1)}, f32[2,256,256]{2,1,0:T(8,128)S(1)}, bf16[2,256,256]{2,1,0:T(8,128)(2,1)S(1)}, bf16[2,256,256]{2,1,0:T(8,128)(2,1)S(1)}, bf16[512,256]{1,0:T(8,128)(2,1)S(1)}) custom-call(bf16[1,512,256]{2,1,0:T(8,128)(2,1)} %grad_hbm.1, s32[1,512]{1,0:T(1,128)} %row_block_hbm.1, s32[1,512]{1,0:T(1,128)} %row_index_hbm.1, ...), custom_call_target="tpu_custom_call" | custom-call | tf_op jit(solution)/shard_map/soap_step/pallas_call | solution.py:312
  41.7 1.3 %keep.1 = (f32[1,2,256,256]{3,2,1,0:T(8,128)}, f32[1,2,256,256]{3,2,1,0:T(8,128)}, bf16[1,2,256,256]{3,2,1,0:T(8,128)(2,1)}, bf16[1,2,256,256]{3,2,1,0:T(8,128)(2,1)}, bf16[1,512,256]{2,1,0:T(8,128)(2,1)}) custom-call(f32[2,256,256]{2,1,0:T(8,128)S(1)} %get-tuple-element.10.refs_0_, f32[2,256,256]{2,1,0:T(8,128)S(1)} %get-tuple-element.11.refs_1_, ...), custom_call_target="tpu_custom_call" | custom-call | tf_op jit(solution)/shard_map/keep/pallas_call | solution.py:367

commit v3 on v2

--- a/solution.py
+++ b/solution.py
@@ -86,6 +86,8 @@
     in_sem,
     send_sem,
     recv_sem,
+    up_sem,
+    down_sem,
 ):
     me = lax.axis_index("fsdp")
     mine = lax.axis_index("grp")
@@ -123,8 +125,10 @@
         load.start()
 
     barrier = pltpu.get_barrier_semaphore()
-    for step in steps(sizes):
-        pl.semaphore_signal(barrier, inc=1, device_id=(peer(step), mine), device_id_type=MESH)
+    row = [(dx, 0, dc) for dx in range(nx) for dc in range(nc) if dx or dc]
+    above, below = peer((0, 1, 0)), peer((0, ny - 1, 0))
+    for to in [above, below] + [peer(step) for step in row]:
+        pl.semaphore_signal(barrier, inc=1, device_id=(to, mine), device_id_type=MESH)
 
     @pl.when(mine == 0)
     def _():
@@ -156,12 +160,21 @@
     @pl.when(mine == 0)
     def _():
         part_in[0] = part_out[...]
-        pl.semaphore_wait(barrier, n - 1)
+        pl.semaphore_wait(barrier, len(row) + 2)
 
     @pl.when(mine != 0)
     def _():
-        pl.semaphore_wait(barrier, n)
+        pl.semaphore_wait(barrier, len(row) + 3)
         send(part_out, part_in.at[mine], 0, (me, 0))
+
+    def pass_up():
+        pl.semaphore_signal(up_sem, inc=1, device_id=(above, mine), device_id_type=MESH)
+
+    def pass_down():
+        pl.semaphore_signal(down_sem, inc=1, device_id=(below, mine), device_id_type=MESH)
+
+    pass_up()
+    pass_down()
 
     for load in loads[1:4]:
         load.wait()
@@ -178,6 +191,16 @@
     to_owner[...] = hot(iota((rows, rows), 0) == owner * PIECE + inner)
     send_a[...] = dot(to_owner[...], grad_v[...]).reshape(n, PIECE, width).astype(jnp.bfloat16)
 
+    ups, downs = ny // 2, ny - 1 - ny // 2
+    for k in range(1, ups + 1):
+        pl.semaphore_wait(up_sem, 1)
+        if k < ups:
+            pass_up()
+        if k <= downs:
+            pl.semaphore_wait(down_sem, 1)
+            if k < downs:
+                pass_down()
+
     to_peers(meta_out, meta_in, 1)
     to_peers(send_a, recv_a, 2)
     meta_in[me] = meta_out[me]
@@ -237,32 +260,36 @@
     def _():
         pltpu.make_async_copy(all_in, all_in, recv_sem.at[4]).wait()
 
-    scale = jnp.minimum(1.0, CLIP_RMS / jnp.sqrt(all_in[...] / entries + 1e-06))[:, 0:1]
-
-    updates = []
-    for b in range(per_owner):
-        basis_l = basis_l_v[b]
-        basis_r = basis_r_v[b]
-        block = (scale * stacked_v[b * width : (b + 1) * width]).astype(jnp.bfloat16)
-        clipped_v[b] = block
-        turned = dot(basis_l_t[b], block).astype(jnp.bfloat16)
-        rotated = dot(turned, basis_r)
-        m = BETA * first_v[b].astype(jnp.float32) + (1.0 - BETA) * rotated
-        v = BETA * second_v[b].astype(jnp.float32) + (1.0 - BETA) * rotated * rotated
+    scale = jnp.minimum(1.0, CLIP_RMS / jnp.sqrt(all_in[...] / entries + 1e-06))
+    scale = jnp.concatenate([scale] * (width // LANES), axis=1)
+
+    every = range(per_owner)
+    clipped = [(scale * stacked_v[b * width : (b + 1) * width]).astype(jnp.bfloat16) for b in every]
+    turned = [dot(basis_l_t[b], clipped[b]).astype(jnp.bfloat16) for b in every]
+    for b in every:
+        clipped_v[b] = clipped[b]
+    rotated = [dot(turned[b], basis_r_v[b]) for b in every]
+    normalized = []
+    for b in every:
+        m = BETA * first_v[b].astype(jnp.float32) + (1.0 - BETA) * rotated[b]
+        v = BETA * second_v[b].astype(jnp.float32) + (1.0 - BETA) * rotated[b] * rotated[b]
         first_out[b] = m.astype(jnp.bfloat16)
         second_out[b] = v.astype(jnp.bfloat16)
-        normalized = (m / (jnp.sqrt(v) + EPS)).astype(jnp.bfloat16)
-        back = dot(basis_l, normalized).astype(jnp.bfloat16)
-        updates.append(dot(back, basis_r, ((1,), (1,))).astype(jnp.bfloat16))
+        normalized.append((m / (jnp.sqrt(v) + EPS)).astype(jnp.bfloat16))
+    back = [dot(basis_l_v[b], normalized[b]).astype(jnp.bfloat16) for b in every]
+    updates = [dot(back[b], basis_r_v[b], ((1,), (1,))).astype(jnp.bfloat16) for b in every]
     update = jnp.concatenate(updates, axis=0)
     send_b[...] = dot(from_state[...], update).reshape(n, PIECE, width).astype(jnp.bfloat16)
     to_peers(send_b, recv_b, 5)
     recv_b[me] = send_b[me]
 
-    for b in range(per_owner):
+    def covariances(b, carry):
         block = clipped_v[b]
         cov_l_out[b] = BETA * cov_l_v[b] + (1.0 - BETA) * dot(block, block, ((1,), (1,)))
         cov_r_out[b] = BETA * cov_r_v[b] + (1.0 - BETA) * dot(block, block, ((0,), (0,)))
+        return carry
+
+    lax.fori_loop(0, per_owner, covariances, 0)
 
     wait_for(meta_out, n - 1, send_sem.at[1])
     wait_for(send_a, n - 1, send_sem.at[2])
@@ -353,6 +380,8 @@
                 pltpu.SemaphoreType.DMA((10,)),
                 pltpu.SemaphoreType.DMA((6,)),
                 pltpu.SemaphoreType.DMA((6,)),
+                pltpu.SemaphoreType.REGULAR,
+                pltpu.SemaphoreType.REGULAR,
             ],
             compiler_params=pltpu.CompilerParams(
                 collective_id=0, has_side_effects=True, vmem_limit_bytes=24 * 1024 * 1024

time: 43.1 us -> 41.1 us (0.954)
  Pallas kernels: 42.3 us -> 40.3 us
    pallas_call x1, Pallas kernels: 41 us -> 39.1 us  [shard(): pl.pallas_call(functools.partial(kernel, entries, sizes, groups), out_sha...]
where the time goes in v3:
time: 41.1 us; the launch traced here: 41 us
  Pallas kernels  40.3 us (98%)
  between operations  0.64 us (2%)
    pallas_call x1, Pallas kernels, shard(): pl.pallas_call(functools.partial(kernel, entries, sizes, groups), out_sha...  39.1 us
    pallas_call x1, Pallas kernels, shard(): pl.pallas_call(keep, out_shape=tuple((jax.ShapeDtypeStruct((1,) + r.shape...  1.27 us

profile of v3, /device:TPU:1, one launch (start us, length us, event | category | flops | bytes accessed | tf_op | source)
XLA Modules:
  0.0 41.0 jit_solution(15116326297830244377)
XLA Ops:
  0.6 39.1 %soap_step.1 = (f32[2,256,256]{2,1,0:T(8,128)S(1)}, f32[2,256,256]{2,1,0:T(8,128)S(1)}, bf16[2,256,256]{2,1,0:T(8,128)(2,1)S(1)}, bf16[2,256,256]{2,1,0:T(8,128)(2,1)S(1)}, bf16[512,256]{1,0:T(8,128)(2,1)S(1)}) custom-call(bf16[1,512,256]{2,1,0:T(8,128)(2,1)} %grad_hbm.1, s32[1,512]{1,0:T(1,128)} %row_block_hbm.1, s32[1,512]{1,0:T(1,128)} %row_index_hbm.1, ...), custom_call_target="tpu_custom_call" | custom-call | tf_op jit(solution)/shard_map/soap_step/pallas_call | solution.py:339
  39.7 1.3 %keep.1 = (f32[1,2,256,256]{3,2,1,0:T(8,128)}, f32[1,2,256,256]{3,2,1,0:T(8,128)}, bf16[1,2,256,256]{3,2,1,0:T(8,128)(2,1)}, bf16[1,2,256,256]{3,2,1,0:T(8,128)(2,1)}, bf16[1,512,256]{2,1,0:T(8,128)(2,1)}) custom-call(f32[2,256,256]{2,1,0:T(8,128)S(1)} %get-tuple-element.10.refs_0_, f32[2,256,256]{2,1,0:T(8,128)S(1)} %get-tuple-element.11.refs_1_, ...), custom_call_target="tpu_custom_call" | custom-call | tf_op jit(solution)/shard_map/keep/pallas_call | solution.py:396

commit v4 on v3

--- a/solution.py
+++ b/solution.py
@@ -28,11 +28,10 @@
     return lax.dot_general(a, b, (dims, ((), ())), preferred_element_type=jnp.float32)
 
 
-def steps(sizes):
-    nx, ny, nc = sizes
-    near_y = sorted(range(ny), key=lambda d: -min(d, ny - d))
-    near_x = sorted(range(nx), key=lambda d: -min(d, nx - d))
-    return [(dx, dy, dc) for dy in near_y for dx in near_x for dc in range(nc) if dx or dy or dc]
+def chip_steps(nx, ny):
+    far_y = sorted(range(ny), key=lambda d: -min(d, ny - d))
+    far_x = sorted(range(nx), key=lambda d: -min(d, nx - d))
+    return [(dx, dy) for dy in far_y for dx in far_x if dx or dy]
 
 
 def kernel(
@@ -83,6 +82,7 @@
     from_owner,
     to_state,
     from_state,
+    grad_sem,
     in_sem,
     send_sem,
     recv_sem,
@@ -99,16 +99,18 @@
     per_block = width // PIECE
     my_x, my_y, my_c = me // (ny * nc), lax.rem(me // nc, ny), lax.rem(me, nc)
 
-    def peer(step):
-        dx, dy, dc = step
-        x, y, c = lax.rem(my_x + dx, nx), lax.rem(my_y + dy, ny), lax.rem(my_c + dc, nc)
-        return (x * ny + y) * nc + c
+    def peer(dx, dy, core):
+        return (lax.rem(my_x + dx, nx) * ny + lax.rem(my_y + dy, ny)) * nc + core
+
+    partner = peer(0, 0, 1 - my_c)
+    far = chip_steps(nx, ny)
+    peers = [peer(dx, dy, core) for core in (1, 0) for dx, dy in far] + [partner]
+    adder = peer(0, 0, 1)
 
     loads = [
         pltpu.make_async_copy(source, target, in_sem.at[i])
         for i, (source, target) in enumerate(
             [
-                (grad_hbm.at[0], grad_v),
                 (row_block_hbm, row_block_v),
                 (home_hbm, home_v),
                 (row_index_hbm, row_index_v),
@@ -121,19 +123,29 @@
             ]
         )
     ]
-    for load in loads:
+    split = 4
+    cut = [pl.ds(i * (rows // split), rows // split) for i in range(split)]
+    grad_loads = [
+        pltpu.make_async_copy(grad_hbm.at[0, part], grad_v.at[part], grad_sem.at[i])
+        for i, part in enumerate(cut)
+    ]
+    for load in grad_loads + loads[:3]:
         load.start()
 
     barrier = pltpu.get_barrier_semaphore()
-    row = [(dx, 0, dc) for dx in range(nx) for dc in range(nc) if dx or dc]
-    above, below = peer((0, 1, 0)), peer((0, ny - 1, 0))
-    for to in [above, below] + [peer(step) for step in row]:
+    row = [partner] + [peer(dx, 0, core) for dx in range(1, nx) for core in range(nc)]
+    above, below = peer(0, 1, my_c), peer(0, ny - 1, my_c)
+    for to in [above, below] + row:
         pl.semaphore_signal(barrier, inc=1, device_id=(to, mine), device_id_type=MESH)
 
-    @pl.when(mine == 0)
+    first_group = mine == 0
+    adds = jnp.logical_and(first_group, my_c == 1)
+
+    @pl.when(adds)
     def _():
         def greet(g, carry):
             pl.semaphore_signal(barrier, inc=1, device_id=(me, g), device_id_type=MESH)
+            pl.semaphore_signal(barrier, inc=1, device_id=(partner, g), device_id_type=MESH)
             return carry
 
         lax.fori_loop(1, groups, greet, 0)
@@ -144,28 +156,38 @@
         ).start()
 
     def to_peers(source, target, k):
-        for step in steps(sizes):
-            to = peer(step)
+        for to in peers:
             send(source.at[to], target.at[me], k, (to, mine))
 
     def wait_for(buffer, count, sem):
         part = buffer.at[pl.ds(0, count)]
         pltpu.make_async_copy(part, part, sem).wait()
 
-    loads[0].wait()
-    wide = grad_v[...].astype(jnp.float32)
-    total = jnp.sum(jnp.sum(wide * wide, axis=0, keepdims=True), axis=1, keepdims=True)
+    squares = jnp.zeros((1, width), jnp.float32)
+    for load, part in zip(grad_loads, cut):
+        load.wait()
+        wide = grad_v[part].astype(jnp.float32)
+        squares += jnp.sum(wide * wide, axis=0, keepdims=True)
+    total = jnp.sum(squares, axis=1, keepdims=True)
     part_out[...] = jnp.broadcast_to(total, (1, LANES))
 
-    @pl.when(mine == 0)
-    def _():
-        part_in[0] = part_out[...]
+    slot = mine * nc + my_c
+
+    @pl.when(first_group)
+    def _():
         pl.semaphore_wait(barrier, len(row) + 2)
 
-    @pl.when(mine != 0)
+    @pl.when(jnp.logical_not(first_group))
     def _():
         pl.semaphore_wait(barrier, len(row) + 3)
-        send(part_out, part_in.at[mine], 0, (me, 0))
+
+    @pl.when(adds)
+    def _():
+        part_in[slot] = part_out[...]
+
+    @pl.when(jnp.logical_not(adds))
+    def _():
+        send(part_out, part_in.at[slot], 0, (adder, 0))
 
     def pass_up():
         pl.semaphore_signal(up_sem, inc=1, device_id=(above, mine), device_id_type=MESH)
@@ -176,7 +198,9 @@
     pass_up()
     pass_down()
 
-    for load in loads[1:4]:
+    for load in loads[3:]:
+        load.start()
+    for load in loads[:3]:
         load.wait()
     lookup = hot(iota((blocks, rows), 0) == row_block_v[...])
     homes = jnp.broadcast_to(home_v[...].astype(jnp.float32), (8, blocks)).astype(jnp.bfloat16)
@@ -214,7 +238,7 @@
     place = spread.astype(jnp.int32) + iota((rows, LANES), 0) % PIECE
     for c in range(rows // LANES):
         from_owner[:, c * LANES : (c + 1) * LANES] = hot(iota((rows, LANES), 1) + c * LANES == place)
-    for load in loads[4:]:
+    for load in loads[3:]:
         load.wait()
     for b in range(per_owner):
         basis_l_t[b] = basis_l_v[b].T
@@ -231,32 +255,41 @@
     )[0:1].astype(jnp.int32)
     to_state[...] = hot(iota((rows, rows), 0) == came_row * PIECE + inner)
 
-    @pl.when(mine == 0)
-    def _():
-        wait_for(part_in, groups - 1, recv_sem.at[0])
+    @pl.when(adds)
+    def _():
+        wait_for(part_in, groups * nc - 1, recv_sem.at[0])
         sum_out[...] = jnp.sum(part_in[:, 0, :], axis=0, keepdims=True)
-        for step in steps(sizes):
-            to = peer(step)
-            send(sum_out, sum_in.at[me], 3, (to, mine))
-        sum_in[me] = sum_out[...]
+        for to in [peer(dx, dy, core) for dx, dy in far for core in range(nc)] + [partner]:
+            send(sum_out, sum_in.at[me // nc], 3, (to, mine))
+        sum_in[me // nc] = sum_out[...]
 
     wait_for(recv_a, n - 1, recv_sem.at[2])
     arrived = recv_a[...].astype(jnp.float32).reshape(rows, width).astype(jnp.bfloat16)
     stacked_v[...] = dot(to_state[...], arrived)
 
-    @pl.when(mine == 0)
-    def _():
-        wait_for(sum_in, n - 1, recv_sem.at[3])
+    @pl.when(adds)
+    def _():
+        wait_for(sum_in, n // nc - 1, recv_sem.at[3])
+
+    @pl.when(jnp.logical_and(first_group, my_c != 1))
+    def _():
+        wait_for(sum_in, n // nc, recv_sem.at[3])
+
+    @pl.when(first_group)
+    def _():
         all_out[...] = jnp.sum(sum_in[:, 0, :], axis=0, keepdims=True)
-
+        all_in[...] = all_out[...]
+
+    @pl.when(adds)
+    def _():
         def tell(g, carry):
+            send(all_out, all_in, 4, (partner, g))
             send(all_out, all_in, 4, (me, g))
             return carry
 
         lax.fori_loop(1, groups, tell, 0)
-        all_in[...] = all_out[...]
-
-    @pl.when(mine != 0)
+
+    @pl.when(jnp.logical_not(first_group))
     def _():
         pltpu.make_async_copy(all_in, all_in, recv_sem.at[4]).wait()
 
@@ -294,12 +327,12 @@
     wait_for(meta_out, n - 1, send_sem.at[1])
     wait_for(send_a, n - 1, send_sem.at[2])
 
-    @pl.when(mine == 0)
-    def _():
-        wait_for(sum_in, n - 1, send_sem.at[3])
-        wait_for(part_in, groups - 1, send_sem.at[4])
-
-    @pl.when(mine != 0)
+    @pl.when(adds)
+    def _():
+        wait_for(meta_in, n - 1, send_sem.at[3])
+        wait_for(part_in, (groups - 1) * nc, send_sem.at[4])
+
+    @pl.when(jnp.logical_not(adds))
     def _():
         pltpu.make_async_copy(part_out, part_out, send_sem.at[0]).wait()
 
@@ -368,16 +401,17 @@
                 vmem((n, 1, LANES), f32),
                 vmem((n, 1, LANES), f32),
                 vmem((1, LANES), f32),
-                vmem((groups, 1, LANES), f32),
+                vmem((groups * sizes[2], 1, LANES), f32),
                 vmem((1, LANES), f32),
-                vmem((n, 1, LANES), f32),
+                vmem((n // sizes[2], 1, LANES), f32),
                 vmem((1, LANES), f32),
                 vmem((1, LANES), f32),
                 vmem((rows, rows), bf16),
                 vmem((rows, rows), bf16),
                 vmem((rows, rows), bf16),
                 vmem((rows, rows), bf16),
-                pltpu.SemaphoreType.DMA((10,)),
+                pltpu.SemaphoreType.DMA((4,)),
+                pltpu.SemaphoreType.DMA((9,)),
                 pltpu.SemaphoreType.DMA((6,)),
                 pltpu.SemaphoreType.DMA((6,)),
                 pltpu.SemaphoreType.REGULAR,

time: 41.1 us -> 40.7 us (level)
  the two profiles are of different devices: /device:TPU:1 before, /device:TPU:64 now
where the time goes in v4:
time: 40.7 us; the launch traced here: 40.5 us
  Pallas kernels  39.8 us (98%)
  between operations  0.64 us (2%)
    pallas_call x1, Pallas kernels, shard(): pl.pallas_call(functools.partial(kernel, entries, sizes, groups), out_sha...  38.6 us
    pallas_call x1, Pallas kernels, shard(): pl.pallas_call(keep, out_shape=tuple((jax.ShapeDtypeStruct((1,) + r.shape...  1.27 us

profile of v4, /device:TPU:64, one launch (start us, length us, event | category | flops | bytes accessed | tf_op | source)
XLA Modules:
  0.0 40.5 jit_solution(7969799551895134285)
XLA Ops:
  0.6 38.6 %soap_step.1 = (f32[2,256,256]{2,1,0:T(8,128)S(1)}, f32[2,256,256]{2,1,0:T(8,128)S(1)}, bf16[2,256,256]{2,1,0:T(8,128)(2,1)S(1)}, bf16[2,256,256]{2,1,0:T(8,128)(2,1)S(1)}, bf16[512,256]{1,0:T(8,128)(2,1)S(1)}) custom-call(bf16[1,512,256]{2,1,0:T(8,128)(2,1)} %grad_hbm.1, s32[1,512]{1,0:T(1,128)} %row_block_hbm.1, s32[1,512]{1,0:T(1,128)} %row_index_hbm.1, ...), custom_call_target="tpu_custom_call" | custom-call | tf_op jit(solution)/shard_map/soap_step/pallas_call | solution.py:372
  39.2 1.3 %keep.1 = (f32[1,2,256,256]{3,2,1,0:T(8,128)}, f32[1,2,256,256]{3,2,1,0:T(8,128)}, bf16[1,2,256,256]{3,2,1,0:T(8,128)(2,1)}, bf16[1,2,256,256]{3,2,1,0:T(8,128)(2,1)}, bf16[1,512,256]{2,1,0:T(8,128)(2,1)}) custom-call(f32[2,256,256]{2,1,0:T(8,128)S(1)} %get-tuple-element.10.refs_0_, f32[2,256,256]{2,1,0:T(8,128)S(1)} %get-tuple-element.11.refs_1_, ...), custom_call_target="tpu_custom_call" | custom-call | tf_op jit(solution)/shard_map/keep/pallas_call | solution.py:430
